TPU v7x, 32 devices: a whole 2x2x4 slice. The times are simulated.
32 devices in a mesh: groups: 1, seq: 1, row: 16 (over z, y, core), col: 2 (over x).
Axes of the slice: x: 2, y: 2, z: 4, core: 2. Of those that a mesh axis runs over, the one named last changes fastest.
Arguments:
- paired_left: bfloat16 [512, 32, 512], P(('groups', 'seq', 'col'), None, 'row'), may hold values from -24 to 24
- paired_right: bfloat16 [512, 32, 512], P(('groups', 'seq', 'row'), None, 'col'), may hold values from -24 to 24
- unpaired_left: bfloat16 [1024, 32, 512], P(('groups', 'seq', 'col'), None, 'row'), may hold values from -24 to 24
- unpaired_right: bfloat16 [1024, 32, 512], P(('groups', 'seq', 'row'), None, 'col'), may hold values from -24 to 24
- out_weight: bfloat16 [1024, 128], replicated, may hold values from -0.1875 to 0.1875
- out_bias: float32 [128], replicated, may hold values from -6 to 6
- chain_lengths: int32 [12], P('groups'), may hold values from 1 to 128, 512 in all
- unpaired_depths: int32 [12], P('groups'), may hold values from 256 to 1024
Outputs:
- pair_update: bfloat16 [512, 512, 128], P(('groups', 'row'), ('col', 'seq'))
Inputs may be any that keep to these rules, and one draw needn't show every extreme that they name: `chain_lengths`: chain lengths sum to 512. `unpaired_depths`: rows of the unpaired MSA at or beyond a chain's depth are padding.
All inputs are finite; a program needn't handle non-finite values.
Results may differ from a plain program's by a relative error of at most 0.0034.
Values may be sent and summed in bfloat16 or wider, within the bound.
A program may use at most 128 MiB of HBM per device.

v0:
```python
import jax
import jax.numpy as jnp
from jax import lax
from jax.sharding import PartitionSpec as P

CHAINS = 12
S_P = 512


def body(
    paired_left,
    paired_right,
    unpaired_left,
    unpaired_right,
    out_weight,
    out_bias,
    chain_lengths,
    unpaired_depths,
):
    left_pair, left_free = (
        lax.all_gather(paired_left, "col", axis=0, tiled=True),
        lax.all_gather(unpaired_left, "col", axis=0, tiled=True),
    )
    right_pair, right_free = (
        lax.all_gather(paired_right, "row", axis=0, tiled=True),
        lax.all_gather(unpaired_right, "row", axis=0, tiled=True),
    )
    rows_here = left_pair.shape[2]
    cols_here = right_pair.shape[2]
    first_row = lax.axis_index("row") * rows_here
    first_col = lax.axis_index("col") * cols_here
    residues = rows_here * lax.axis_size("row")
    positions = jnp.arange(residues, dtype=jnp.int32)
    chain_ends = jnp.cumsum(chain_lengths)
    chain_of = jnp.sum((positions[:, None] >= chain_ends[None, :]).astype(jnp.int32), axis=1)
    onehot = chain_of[:, None] == jnp.arange(CHAINS, dtype=jnp.int32)[None, :]
    depth_of = jnp.sum(jnp.where(onehot, unpaired_depths[None, :], 0), axis=1)
    chain_rows = lax.dynamic_slice_in_dim(chain_of, first_row, rows_here, 0)
    depth_rows = lax.dynamic_slice_in_dim(depth_of, first_row, rows_here, 0)
    chain_cols = lax.dynamic_slice_in_dim(chain_of, first_col, cols_here, 0)
    free_count = left_free.shape[0]
    free_ids = lax.axis_index("seq") * free_count + jnp.arange(free_count, dtype=jnp.int32)
    live_rows = (free_ids[:, None] < depth_rows[None, :]).astype(left_free.dtype)
    left_free = left_free * live_rows[:, None, :]
    same_chain = (chain_rows[:, None] == chain_cols[None, :]).astype(jnp.float32)
    block_rows = 4
    channels = out_weight.shape[1]

    def one_block(block_index):
        offset = block_index * block_rows
        left_block = lax.dynamic_slice_in_dim(left_pair, offset, block_rows, 2)
        free_block = lax.dynamic_slice_in_dim(left_free, offset, block_rows, 2)
        same_block = lax.dynamic_slice_in_dim(same_chain, offset, block_rows, 0)
        paired = jnp.einsum(
            "sci,sdj->ijcd", left_block, right_pair, preferred_element_type=jnp.float32
        )
        unpaired = jnp.einsum(
            "sci,sdj->ijcd", free_block, right_free, preferred_element_type=jnp.float32
        )
        unpaired = unpaired * same_block[:, :, None, None]
        outer_product = (paired + unpaired).astype(jnp.bfloat16).reshape(block_rows * cols_here, -1)
        projected = jnp.dot(outer_product, out_weight, preferred_element_type=jnp.float32)
        return projected.reshape(block_rows, cols_here, channels)

    projected = lax.map(one_block, jnp.arange(rows_here // block_rows, dtype=jnp.int32))
    projected = projected.reshape(rows_here, cols_here, channels)
    half_cols = cols_here // lax.axis_size("seq")
    own_offset = lax.axis_index("seq") * half_cols
    summed = lax.psum(projected, "seq")
    own_share = lax.dynamic_slice_in_dim(summed, own_offset, half_cols, 1)
    same_share = lax.dynamic_slice_in_dim(same_chain, own_offset, half_cols, 1)
    denominator = S_P + same_share * depth_rows[:, None].astype(jnp.float32)
    return (own_share / denominator[:, :, None] + out_bias).astype(jnp.bfloat16)


def solution(mesh):
    return jax.shard_map(
        body,
        mesh=mesh,
        in_specs=(
            P(("groups", "seq", "col"), None, "row"),
            P(("groups", "seq", "row"), None, "col"),
            P(("groups", "seq", "col"), None, "row"),
            P(("groups", "seq", "row"), None, "col"),
            P(),
            P(),
            P("groups"),
            P("groups"),
        ),
        out_specs=P(("groups", "row"), ("col", "seq"), None),
        check_vma=False,
    )
```

profile of v0, /device:TPU:0, one launch (start us, length us, event | category | flops | bytes accessed | tf_op | source)
XLA Modules:
  0.0 418.2 jit_solution(13821288054562423677)
XLA Ops:
  6.5 2.9 copy.23
  9.5 2.2 copy.21
  11.7 1.1 copy.22
  12.9 1.6 copy.24
  15.4 30.0 %all-gather.9.cloned.1.call-done = bf16[1024,32,32]{0,1,2:T(8,128)(2,1)} async-done(((bf16[512,32,32]{0,1,2:T(8,128)(2,1)}), bf16[1024,32,32]{0,1,2:T(8,128)(2,1)}) %all-gather.9.cloned.1.call-update) | async-done | bytes 2097168 | tf_op jit(solution)/shard_map/all_gather | solution.py:22
  45.4 1.7 broadcast_multiply_fusion
  47.2 21.1 %all-gather.5.cloned.1.call-done = bf16[512,32,32]{0,1,2:T(8,128)(2,1)} async-done(((bf16[256,32,32]{0,1,2:T(8,128)(2,1)}), bf16[512,32,32]{0,1,2:T(8,128)(2,1)}) %all-gather.5.cloned.1.call-update) | async-done | bytes 1048592 | tf_op jit(solution)/shard_map/all_gather | solution.py:21
  68.2 76.5 %all-gather.7.cloned.1.call-done = bf16[512,32,256]{2,0,1:T(8,128)(2,1)} async-done(((bf16[32,32,256]{2,0,1:T(8,128)(2,1)}), bf16[512,32,256]{2,0,1:T(8,128)(2,1)}) %all-gather.7.cloned.1.call-update) | async-done | bytes 8388624 | tf_op jit(solution)/shard_map/all_gather | solution.py:25
  144.8 127.1 %all-gather.11.cloned.1.call-done = bf16[1024,32,256]{2,0,1:T(8,128)(2,1)} async-done(((bf16[64,32,256]{2,0,1:T(8,128)(2,1)}), bf16[1024,32,256]{2,0,1:T(8,128)(2,1)}) %all-gather.11.cloned.1.call-update) | async-done | bytes 16777232 | tf_op jit(solution)/shard_map/all_gather | solution.py:26
  271.9 135.9 %while.10 = (s32[]{:T(128)}, f32[8,4,256,128]{3,2,1,0:T(8,128)}, s32[8]{0:T(128)S(1)}, bf16[512,32,32]{0,1,2:T(8,128)(2,1)}, bf16[512,32,256]{2,0,1:T(8,128)(2,1...) while((s32[]{:T(128)}, f32[8,4,256,128]{3,2,1,0:T(8,128)}, ...), condition=%wide.region_4.5_spmd, body=%wide.region_3.4_spmd.sunk | while | flops 3492806656 | bytes 43135680 | solution.py:65
  271.9 0.6 dynamic_slice.44
  273.1 4.7 %fusion.36 = f32[32,4,32,256]{3,0,2,1:T(8,128)S(1)} fusion(bf16[512,32,256]{2,0,1:T(8,128)(2,1)} %get-tuple-element.158, bf16[512,32,32]{0,1,2:T(8,128)(2,1)} %get-tuple-element.157, s32[]{:T(128)S(6)} %select_n.23), kind=kOutput, calls=%fused_computation.2.clone.1 | convolution fusion | flops 1073741824 | bytes 12713988 | tf_op jit(solution)/shard_map/while/body/eval_jaxpr/sci,sdj->ijcd/dot_general | solution.py:54
  277.9 8.2 %fusion.37 = bf16[4,256,32,32]{1,2,3,0:T(8,128)(2,1)S(1)} fusion(f32[32,4,32,256]{3,0,2,1:T(8,128)S(1)} %fusion.36, f32[4,256]{1,0:T(4,128)S(1)} %constant_dynamic-slice_fusion.2, bf16[1024,32,256]{2,0,1:T(8,128)(2,1)} %get-tuple-element.160, bf16[1024,32,32]{0,1,2:T(8,128)(2,1)S(1)} %get-tuple-element.159, s32[]{:T(128)S(6)} %select_n.23), kind=kOutput, calls=%fused_computation.5.clone.1 | convolution fusion | flops 2150629376 | bytes 23334916 | tf_op jit(solution)/shard_map/while/body/eval_jaxpr/sci,sdj->ijcd/dot_general | solution.py:57
  286.1 1.2 copy.29
  287.3 1.6 fusion.38
  288.9 0.6 dynamic_slice.44
  290.1 4.7 %fusion.36 = f32[32,4,32,256]{3,0,2,1:T(8,128)S(1)} fusion(bf16[512,32,256]{2,0,1:T(8,128)(2,1)} %get-tuple-element.158, bf16[512,32,32]{0,1,2:T(8,128)(2,1)} %get-tuple-element.157, s32[]{:T(128)S(6)} %select_n.23), kind=kOutput, calls=%fused_computation.2.clone.1 | convolution fusion | flops 1073741824 | bytes 12713988 | tf_op jit(solution)/shard_map/while/body/eval_jaxpr/sci,sdj->ijcd/dot_general | solution.py:54
  294.9 8.2 %fusion.37 = bf16[4,256,32,32]{1,2,3,0:T(8,128)(2,1)S(1)} fusion(f32[32,4,32,256]{3,0,2,1:T(8,128)S(1)} %fusion.36, f32[4,256]{1,0:T(4,128)S(1)} %constant_dynamic-slice_fusion.2, bf16[1024,32,256]{2,0,1:T(8,128)(2,1)} %get-tuple-element.160, bf16[1024,32,32]{0,1,2:T(8,128)(2,1)S(1)} %get-tuple-element.159, s32[]{:T(128)S(6)} %select_n.23), kind=kOutput, calls=%fused_computation.5.clone.1 | convolution fusion | flops 2150629376 | bytes 23334916 | tf_op jit(solution)/shard_map/while/body/eval_jaxpr/sci,sdj->ijcd/dot_general | solution.py:57
  303.1 1.2 copy.29
  304.3 1.6 fusion.38
  305.9 0.6 dynamic_slice.44
  307.2 4.7 %fusion.36 = f32[32,4,32,256]{3,0,2,1:T(8,128)S(1)} fusion(bf16[512,32,256]{2,0,1:T(8,128)(2,1)} %get-tuple-element.158, bf16[512,32,32]{0,1,2:T(8,128)(2,1)} %get-tuple-element.157, s32[]{:T(128)S(6)} %select_n.23), kind=kOutput, calls=%fused_computation.2.clone.1 | convolution fusion | flops 1073741824 | bytes 12713988 | tf_op jit(solution)/shard_map/while/body/eval_jaxpr/sci,sdj->ijcd/dot_general | solution.py:54
  311.9 8.2 %fusion.37 = bf16[4,256,32,32]{1,2,3,0:T(8,128)(2,1)S(1)} fusion(f32[32,4,32,256]{3,0,2,1:T(8,128)S(1)} %fusion.36, f32[4,256]{1,0:T(4,128)S(1)} %constant_dynamic-slice_fusion.2, bf16[1024,32,256]{2,0,1:T(8,128)(2,1)} %get-tuple-element.160, bf16[1024,32,32]{0,1,2:T(8,128)(2,1)S(1)} %get-tuple-element.159, s32[]{:T(128)S(6)} %select_n.23), kind=kOutput, calls=%fused_computation.5.clone.1 | convolution fusion | flops 2150629376 | bytes 23334916 | tf_op jit(solution)/shard_map/while/body/eval_jaxpr/sci,sdj->ijcd/dot_general | solution.py:57
  320.1 1.2 copy.29
  321.3 1.6 fusion.38
  322.9 0.6 dynamic_slice.44
  324.1 4.7 %fusion.36 = f32[32,4,32,256]{3,0,2,1:T(8,128)S(1)} fusion(bf16[512,32,256]{2,0,1:T(8,128)(2,1)} %get-tuple-element.158, bf16[512,32,32]{0,1,2:T(8,128)(2,1)} %get-tuple-element.157, s32[]{:T(128)S(6)} %select_n.23), kind=kOutput, calls=%fused_computation.2.clone.1 | convolution fusion | flops 1073741824 | bytes 12713988 | tf_op jit(solution)/shard_map/while/body/eval_jaxpr/sci,sdj->ijcd/dot_general | solution.py:54
  328.9 8.2 %fusion.37 = bf16[4,256,32,32]{1,2,3,0:T(8,128)(2,1)S(1)} fusion(f32[32,4,32,256]{3,0,2,1:T(8,128)S(1)} %fusion.36, f32[4,256]{1,0:T(4,128)S(1)} %constant_dynamic-slice_fusion.2, bf16[1024,32,256]{2,0,1:T(8,128)(2,1)} %get-tuple-element.160, bf16[1024,32,32]{0,1,2:T(8,128)(2,1)S(1)} %get-tuple-element.159, s32[]{:T(128)S(6)} %select_n.23), kind=kOutput, calls=%fused_computation.5.clone.1 | convolution fusion | flops 2150629376 | bytes 23334916 | tf_op jit(solution)/shard_map/while/body/eval_jaxpr/sci,sdj->ijcd/dot_general | solution.py:57
  337.1 1.2 copy.29
  338.3 1.6 fusion.38
  339.9 0.6 dynamic_slice.44
  341.1 4.7 %fusion.36 = f32[32,4,32,256]{3,0,2,1:T(8,128)S(1)} fusion(bf16[512,32,256]{2,0,1:T(8,128)(2,1)} %get-tuple-element.158, bf16[512,32,32]{0,1,2:T(8,128)(2,1)} %get-tuple-element.157, s32[]{:T(128)S(6)} %select_n.23), kind=kOutput, calls=%fused_computation.2.clone.1 | convolution fusion | flops 1073741824 | bytes 12713988 | tf_op jit(solution)/shard_map/while/body/eval_jaxpr/sci,sdj->ijcd/dot_general | solution.py:54
  345.9 8.2 %fusion.37 = bf16[4,256,32,32]{1,2,3,0:T(8,128)(2,1)S(1)} fusion(f32[32,4,32,256]{3,0,2,1:T(8,128)S(1)} %fusion.36, f32[4,256]{1,0:T(4,128)S(1)} %constant_dynamic-slice_fusion.2, bf16[1024,32,256]{2,0,1:T(8,128)(2,1)} %get-tuple-element.160, bf16[1024,32,32]{0,1,2:T(8,128)(2,1)S(1)} %get-tuple-element.159, s32[]{:T(128)S(6)} %select_n.23), kind=kOutput, calls=%fused_computation.5.clone.1 | convolution fusion | flops 2150629376 | bytes 23334916 | tf_op jit(solution)/shard_map/while/body/eval_jaxpr/sci,sdj->ijcd/dot_general | solution.py:57
  354.1 1.2 copy.29
  355.3 1.6 fusion.38
  358.1 4.7 %fusion.36 = f32[32,4,32,256]{3,0,2,1:T(8,128)S(1)} fusion(bf16[512,32,256]{2,0,1:T(8,128)(2,1)} %get-tuple-element.158, bf16[512,32,32]{0,1,2:T(8,128)(2,1)} %get-tuple-element.157, s32[]{:T(128)S(6)} %select_n.23), kind=kOutput, calls=%fused_computation.2.clone.1 | convolution fusion | flops 1073741824 | bytes 12713988 | tf_op jit(solution)/shard_map/while/body/eval_jaxpr/sci,sdj->ijcd/dot_general | solution.py:54
  362.9 8.2 %fusion.37 = bf16[4,256,32,32]{1,2,3,0:T(8,128)(2,1)S(1)} fusion(f32[32,4,32,256]{3,0,2,1:T(8,128)S(1)} %fusion.36, f32[4,256]{1,0:T(4,128)S(1)} %constant_dynamic-slice_fusion.2, bf16[1024,32,256]{2,0,1:T(8,128)(2,1)} %get-tuple-element.160, bf16[1024,32,32]{0,1,2:T(8,128)(2,1)S(1)} %get-tuple-element.159, s32[]{:T(128)S(6)} %select_n.23), kind=kOutput, calls=%fused_computation.5.clone.1 | convolution fusion | flops 2150629376 | bytes 23334916 | tf_op jit(solution)/shard_map/while/body/eval_jaxpr/sci,sdj->ijcd/dot_general | solution.py:57
  371.1 1.2 copy.29
  372.3 1.5 fusion.38
  375.1 4.7 %fusion.36 = f32[32,4,32,256]{3,0,2,1:T(8,128)S(1)} fusion(bf16[512,32,256]{2,0,1:T(8,128)(2,1)} %get-tuple-element.158, bf16[512,32,32]{0,1,2:T(8,128)(2,1)} %get-tuple-element.157, s32[]{:T(128)S(6)} %select_n.23), kind=kOutput, calls=%fused_computation.2.clone.1 | convolution fusion | flops 1073741824 | bytes 12713988 | tf_op jit(solution)/shard_map/while/body/eval_jaxpr/sci,sdj->ijcd/dot_general | solution.py:54
  379.8 8.2 %fusion.37 = bf16[4,256,32,32]{1,2,3,0:T(8,128)(2,1)S(1)} fusion(f32[32,4,32,256]{3,0,2,1:T(8,128)S(1)} %fusion.36, f32[4,256]{1,0:T(4,128)S(1)} %constant_dynamic-slice_fusion.2, bf16[1024,32,256]{2,0,1:T(8,128)(2,1)} %get-tuple-element.160, bf16[1024,32,32]{0,1,2:T(8,128)(2,1)S(1)} %get-tuple-element.159, s32[]{:T(128)S(6)} %select_n.23), kind=kOutput, calls=%fused_computation.5.clone.1 | convolution fusion | flops 2150629376 | bytes 23334916 | tf_op jit(solution)/shard_map/while/body/eval_jaxpr/sci,sdj->ijcd/dot_general | solution.py:57
  388.1 1.2 copy.29
  389.3 1.6 fusion.38
  392.1 4.7 %fusion.36 = f32[32,4,32,256]{3,0,2,1:T(8,128)S(1)} fusion(bf16[512,32,256]{2,0,1:T(8,128)(2,1)} %get-tuple-element.158, bf16[512,32,32]{0,1,2:T(8,128)(2,1)} %get-tuple-element.157, s32[]{:T(128)S(6)} %select_n.23), kind=kOutput, calls=%fused_computation.2.clone.1 | convolution fusion | flops 1073741824 | bytes 12713988 | tf_op jit(solution)/shard_map/while/body/eval_jaxpr/sci,sdj->ijcd/dot_general | solution.py:54
  396.8 8.2 %fusion.37 = bf16[4,256,32,32]{1,2,3,0:T(8,128)(2,1)S(1)} fusion(f32[32,4,32,256]{3,0,2,1:T(8,128)S(1)} %fusion.36, f32[4,256]{1,0:T(4,128)S(1)} %constant_dynamic-slice_fusion.2, bf16[1024,32,256]{2,0,1:T(8,128)(2,1)} %get-tuple-element.160, bf16[1024,32,32]{0,1,2:T(8,128)(2,1)S(1)} %get-tuple-element.159, s32[]{:T(128)S(6)} %select_n.23), kind=kOutput, calls=%fused_computation.5.clone.1 | convolution fusion | flops 2150629376 | bytes 23334916 | tf_op jit(solution)/shard_map/while/body/eval_jaxpr/sci,sdj->ijcd/dot_general | solution.py:57
  405.0 1.2 copy.29
  406.2 1.6 fusion.38
  407.8 3.8 fusion.16
  (42 shorter events, 2.9 us)
Async XLA Ops:
  6.5 5.2 %copy-start.2 = (bf16[32,32,256]{2,1,0:T(8,128)(2,1)S(1)}, bf16[32,32,256]{2,1,0:T(8,128)(2,1)}, u32[]{:S(2)}) copy-start(bf16[32,32,256]{2,1,0:T(8,128)(2,1)} %param.11) | copy-start | bytes 1572868
  6.5 6.4 %copy-start.1 = (bf16[64,32,256]{2,1,0:T(8,128)(2,1)S(1)}, bf16[64,32,256]{2,1,0:T(8,128)(2,1)}, u32[]{:S(2)}) copy-start(bf16[64,32,256]{2,1,0:T(8,128)(2,1)} %param.13) | copy-start | bytes 3145732
  6.5 38.9 %all-gather.9.cloned.1.call-start = ((), (), s32[]{:S(2)}) async-start(), calls=%async_computation.2 | async-start | bytes 3145728 | tf_op jit(solution)/shard_map/all_gather | solution.py:22
  9.4 5.1 %copy-start.5 = (s32[12]{0:T(128)S(1)}, s32[12]{0:T(128)}, u32[]{:S(2)}) copy-start(s32[12]{0:T(128)} %param.16) | copy-start | bytes 148
  9.4 5.6 %copy-start.4 = (s32[12]{0:T(128)S(1)}, s32[12]{0:T(128)}, u32[]{:S(2)}) copy-start(s32[12]{0:T(128)} %param.17) | copy-start | bytes 148
  9.5 58.8 %all-gather.5.cloned.1.call-start = ((), (), s32[]{:S(2)}) async-start(), calls=%async_computation | async-start | bytes 1572864 | tf_op jit(solution)/shard_map/all_gather | solution.py:21
  11.7 133.1 %all-gather.7.cloned.1.call-start = ((), (), s32[]{:S(2)}) async-start(), calls=%async_computation.1 | async-start | bytes 8912896 | tf_op jit(solution)/shard_map/all_gather | solution.py:25
  12.9 259.0 %copy-start = (bf16[1024,128]{1,0:T(8,128)(2,1)S(1)}, bf16[1024,128]{1,0:T(8,128)(2,1)}, u32[]{:S(2)}) copy-start(bf16[1024,128]{1,0:T(8,128)(2,1)} %param.14) | copy-start | bytes 786436
  12.9 259.0 %all-gather.11.cloned.1.call-start = ((), (), s32[]{:S(2)}) async-start(), calls=%async_computation.3 | async-start | bytes 17825792 | tf_op jit(solution)/shard_map/all_gather | solution.py:26
  271.9 135.9 %copy-start.3 = (f32[128]{0:T(128)S(1)}, f32[128]{0:T(128)}, u32[]{:S(2)}) copy-start(f32[128]{0:T(128)} %param.15) | copy-start | bytes 1540
Sparse Core Ops, SparseCore 0:
  9.6 35.8 all-gather.8
  47.0 21.2 all-gather.4
  70.4 74.3 all-gather.6
  146.8 125.0 all-gather.10
where the time goes:
time: 419 us; the launch traced here: 418 us
  waiting for transfers between devices  255 us (61%)
  matrix products  116 us (28%)
  local copies, waits for them, and re-layouts  22.2 us (5%)
  between operations  13.2 us (3%)
  other arithmetic  6.23 us (1%)
  loops' own time  5.49 us (1%)
    all_gather x1, waiting for transfers between devices, body(): lax.all_gather(unpaired_right, 'row', axis=0, tiled=True)  127 us
    all_gather x1, waiting for transfers between devices, body(): lax.all_gather(paired_right, 'row', axis=0, tiled=True)  76.5 us
    dot_general x8, matrix products, one_block(): jnp.einsum('sci,sdj->ijcd', free_block, right_free, preferred_element_typ...  65.7 us
    dot_general x8, matrix products, one_block(): jnp.einsum('sci,sdj->ijcd', left_block, right_pair, preferred_element_typ...  37.9 us
    all_gather x1, waiting for transfers between devices, body(): lax.all_gather(unpaired_left, 'col', axis=0, tiled=True)  30 us
    all_gather x1, waiting for transfers between devices, body(): lax.all_gather(paired_left, 'col', axis=0, tiled=True)  21.1 us
    dot_general x8, matrix products, one_block(): jnp.dot(outer_product, out_weight, preferred_element_type=jnp.float32)  12.6 us
    convert_element_type x8, local copies, waits for them, and re-layouts, one_block(): (paired + unpaired).astype(jnp.bfloat16).reshape(block_rows * cols_here, -1)  9.51 us
  transfers between devices with their start and end apart: 4, of which 4 were waited for; matrix products, arithmetic and copies ran while one was open for 2% of the time, Pallas kernels for 0%

commit v1 on v0

--- a/solution.py
+++ b/solution.py
@@ -18,7 +18,13 @@
     unpaired_depths,
 ):
     left_pair, left_free = (
-        lax.all_gather(paired_left, "col", axis=0, tiled=True),
+        jnp.roll(
+            jnp.concatenate(
+                [paired_left, lax.ppermute(paired_left, "col", [(0, 1), (1, 0)])], axis=0
+            ),
+            lax.axis_index("col") * paired_left.shape[0],
+            axis=0,
+        ),
         lax.all_gather(unpaired_left, "col", axis=0, tiled=True),
     )
     right_pair, right_free = (

time: 419 us -> 404 us (0.964)
  waiting for transfers between devices: 255 us -> 236 us
    all_gather x1 -> x0, waiting for transfers between devices: 21.1 us -> none  [body(): lax.all_gather(paired_left, 'col', axis=0, tiled=True)]
    ppermute x0 -> x1, waiting for transfers between devices: none -> 18.7 us  [body(): lax.ppermute(paired_left, 'col', [(0, 1), (1, 0)])]
    all_gather x1, waiting for transfers between devices: 30 us -> 14.1 us  [body(): lax.all_gather(unpaired_left, 'col', axis=0, tiled=True)]
where the time goes in v1:
time: 404 us; the launch traced here: 403 us
  waiting for transfers between devices  236 us (58%)
  matrix products  116 us (29%)
  local copies, waits for them, and re-layouts  21.5 us (5%)
  between operations  13.2 us (3%)
  other arithmetic  7.16 us (2%)
  loops' own time  5.45 us (1%)
    all_gather x1, waiting for transfers between devices, body(): lax.all_gather(unpaired_right, 'row', axis=0, tiled=True)  127 us
    all_gather x1, waiting for transfers between devices, body(): lax.all_gather(paired_right, 'row', axis=0, tiled=True)  76.3 us
    dot_general x8, matrix products, one_block(): jnp.einsum('sci,sdj->ijcd', free_block, right_free, preferred_element_typ...  66.7 us
    dot_general x8, matrix products, one_block(): jnp.einsum('sci,sdj->ijcd', left_block, right_pair, preferred_element_typ...  37.3 us
    ppermute x1, waiting for transfers between devices, body(): lax.ppermute(paired_left, 'col', [(0, 1), (1, 0)])  18.7 us
    all_gather x1, waiting for transfers between devices, body(): lax.all_gather(unpaired_left, 'col', axis=0, tiled=True)  14.1 us
    dot_general x8, matrix products, one_block(): jnp.dot(outer_product, out_weight, preferred_element_type=jnp.float32)  12.5 us
    convert_element_type x8, local copies, waits for them, and re-layouts, one_block(): (paired + unpaired).astype(jnp.bfloat16).reshape(block_rows * cols_here, -1)  9.64 us
  transfers between devices with their start and end apart: 4, of which 4 were waited for; matrix products, arithmetic and copies ran while one was open for 2% of the time, Pallas kernels for 0%

profile of v1, /device:TPU:0, one launch (start us, length us, event | category | flops | bytes accessed | tf_op | source)
XLA Modules:
  0.0 403.3 jit_solution(5642110555012061895)
XLA Ops:
  6.6 2.9 copy.29
  9.5 2.1 copy.28
  11.8 1.6 copy.30
  13.7 3.0 collective-permute-start
  17.5 18.7 %collective-permute-done = bf16[256,32,32]{0,1,2:T(8,128)(2,1)S(1)} collective-permute-done((bf16[256,32,32]{0,1,2:T(8,128)(2,1)S(1)}, bf16[256,32,32]{0,1,2:T(8,128)(2,1)S(1)}, u32[]{:S(2)}, u32[]{:S(2)}) %collective-permute-start) | collective-permute-done | bytes 524320 | tf_op jit(solution)/shard_map/ppermute | solution.py:23
  36.3 0.9 fusion.19
  37.2 14.1 %all-gather.6.cloned.1.call-done = bf16[1024,32,32]{0,1,2:T(8,128)(2,1)} async-done(((bf16[512,32,32]{0,1,2:T(8,128)(2,1)}), bf16[1024,32,32]{0,1,2:T(8,128)(2,1)}) %all-gather.6.cloned.1.call-update) | async-done | bytes 2097168 | tf_op jit(solution)/shard_map/all_gather | solution.py:28
  51.3 1.7 broadcast_multiply_fusion
  53.1 76.3 %all-gather.4.cloned.1.call-done = bf16[512,32,256]{2,0,1:T(8,128)(2,1)} async-done(((bf16[32,32,256]{2,0,1:T(8,128)(2,1)}), bf16[512,32,256]{2,0,1:T(8,128)(2,1)}) %all-gather.4.cloned.1.call-update) | async-done | bytes 8388624 | tf_op jit(solution)/shard_map/all_gather | solution.py:31
  129.4 127.3 %all-gather.8.cloned.1.call-done = bf16[1024,32,256]{2,0,1:T(8,128)(2,1)} async-done(((bf16[64,32,256]{2,0,1:T(8,128)(2,1)}), bf16[1024,32,256]{2,0,1:T(8,128)(2,1)}) %all-gather.8.cloned.1.call-update) | async-done | bytes 16777232 | tf_op jit(solution)/shard_map/all_gather | solution.py:32
  256.6 136.3 %while.10 = (s32[]{:T(128)}, f32[8,4,256,128]{3,2,1,0:T(8,128)}, s32[8]{0:T(128)S(1)}, bf16[512,32,32]{0,1,2:T(8,128)(2,1)S(1)}, bf16[512,32,256]{2,0,1:T(8,128)...) while((s32[]{:T(128)}, f32[8,4,256,128]{3,2,1,0:T(8,128)}, ...), condition=%wide.region_4.5_spmd, body=%wide.region_3.4_spmd.sunk | while | flops 3492806656 | bytes 43135680 | solution.py:71
  256.6 0.6 dynamic_slice.69
  257.9 4.7 %fusion.39 = f32[32,4,32,256]{3,0,2,1:T(8,128)S(1)} fusion(bf16[512,32,256]{2,0,1:T(8,128)(2,1)} %get-tuple-element.158, bf16[512,32,32]{0,1,2:T(8,128)(2,1)S(1)} %get-tuple-element.157, s32[]{:T(128)S(6)} %select_n.38), kind=kOutput, calls=%fused_computation.2.clone.1 | convolution fusion | flops 1073741824 | bytes 12713988 | tf_op jit(solution)/shard_map/while/body/eval_jaxpr/sci,sdj->ijcd/dot_general | solution.py:60
  262.6 8.3 %fusion.40 = bf16[4,256,32,32]{1,2,3,0:T(8,128)(2,1)S(1)} fusion(f32[32,4,32,256]{3,0,2,1:T(8,128)S(1)} %fusion.39, f32[4,256]{1,0:T(4,128)S(1)} %constant_dynamic-slice_fusion.2, bf16[1024,32,256]{2,0,1:T(8,128)(2,1)} %get-tuple-element.160, bf16[1024,32,32]{0,1,2:T(8,128)(2,1)S(1)} %get-tuple-element.159, s32[]{:T(128)S(6)} %select_n.38), kind=kOutput, calls=%fused_computation.5.clone.1 | convolution fusion | flops 2150629376 | bytes 23334916 | tf_op jit(solution)/shard_map/while/body/eval_jaxpr/sci,sdj->ijcd/dot_general | solution.py:63
  270.9 1.2 copy.35
  272.1 1.6 fusion.41
  273.7 0.6 dynamic_slice.69
  275.0 4.7 %fusion.39 = f32[32,4,32,256]{3,0,2,1:T(8,128)S(1)} fusion(bf16[512,32,256]{2,0,1:T(8,128)(2,1)} %get-tuple-element.158, bf16[512,32,32]{0,1,2:T(8,128)(2,1)S(1)} %get-tuple-element.157, s32[]{:T(128)S(6)} %select_n.38), kind=kOutput, calls=%fused_computation.2.clone.1 | convolution fusion | flops 1073741824 | bytes 12713988 | tf_op jit(solution)/shard_map/while/body/eval_jaxpr/sci,sdj->ijcd/dot_general | solution.py:60
  279.6 8.3 %fusion.40 = bf16[4,256,32,32]{1,2,3,0:T(8,128)(2,1)S(1)} fusion(f32[32,4,32,256]{3,0,2,1:T(8,128)S(1)} %fusion.39, f32[4,256]{1,0:T(4,128)S(1)} %constant_dynamic-slice_fusion.2, bf16[1024,32,256]{2,0,1:T(8,128)(2,1)} %get-tuple-element.160, bf16[1024,32,32]{0,1,2:T(8,128)(2,1)S(1)} %get-tuple-element.159, s32[]{:T(128)S(6)} %select_n.38), kind=kOutput, calls=%fused_computation.5.clone.1 | convolution fusion | flops 2150629376 | bytes 23334916 | tf_op jit(solution)/shard_map/while/body/eval_jaxpr/sci,sdj->ijcd/dot_general | solution.py:63
  288.0 1.2 copy.35
  289.2 1.6 fusion.41
  290.8 0.6 dynamic_slice.69
  292.0 4.7 %fusion.39 = f32[32,4,32,256]{3,0,2,1:T(8,128)S(1)} fusion(bf16[512,32,256]{2,0,1:T(8,128)(2,1)} %get-tuple-element.158, bf16[512,32,32]{0,1,2:T(8,128)(2,1)S(1)} %get-tuple-element.157, s32[]{:T(128)S(6)} %select_n.38), kind=kOutput, calls=%fused_computation.2.clone.1 | convolution fusion | flops 1073741824 | bytes 12713988 | tf_op jit(solution)/shard_map/while/body/eval_jaxpr/sci,sdj->ijcd/dot_general | solution.py:60
  296.7 8.3 %fusion.40 = bf16[4,256,32,32]{1,2,3,0:T(8,128)(2,1)S(1)} fusion(f32[32,4,32,256]{3,0,2,1:T(8,128)S(1)} %fusion.39, f32[4,256]{1,0:T(4,128)S(1)} %constant_dynamic-slice_fusion.2, bf16[1024,32,256]{2,0,1:T(8,128)(2,1)} %get-tuple-element.160, bf16[1024,32,32]{0,1,2:T(8,128)(2,1)S(1)} %get-tuple-element.159, s32[]{:T(128)S(6)} %select_n.38), kind=kOutput, calls=%fused_computation.5.clone.1 | convolution fusion | flops 2150629376 | bytes 23334916 | tf_op jit(solution)/shard_map/while/body/eval_jaxpr/sci,sdj->ijcd/dot_general | solution.py:63
  305.1 1.2 copy.35
  306.3 1.6 fusion.41
  309.1 4.7 %fusion.39 = f32[32,4,32,256]{3,0,2,1:T(8,128)S(1)} fusion(bf16[512,32,256]{2,0,1:T(8,128)(2,1)} %get-tuple-element.158, bf16[512,32,32]{0,1,2:T(8,128)(2,1)S(1)} %get-tuple-element.157, s32[]{:T(128)S(6)} %select_n.38), kind=kOutput, calls=%fused_computation.2.clone.1 | convolution fusion | flops 1073741824 | bytes 12713988 | tf_op jit(solution)/shard_map/while/body/eval_jaxpr/sci,sdj->ijcd/dot_general | solution.py:60
  313.7 8.3 %fusion.40 = bf16[4,256,32,32]{1,2,3,0:T(8,128)(2,1)S(1)} fusion(f32[32,4,32,256]{3,0,2,1:T(8,128)S(1)} %fusion.39, f32[4,256]{1,0:T(4,128)S(1)} %constant_dynamic-slice_fusion.2, bf16[1024,32,256]{2,0,1:T(8,128)(2,1)} %get-tuple-element.160, bf16[1024,32,32]{0,1,2:T(8,128)(2,1)S(1)} %get-tuple-element.159, s32[]{:T(128)S(6)} %select_n.38), kind=kOutput, calls=%fused_computation.5.clone.1 | convolution fusion | flops 2150629376 | bytes 23334916 | tf_op jit(solution)/shard_map/while/body/eval_jaxpr/sci,sdj->ijcd/dot_general | solution.py:63
  322.1 1.2 copy.35
  323.3 1.5 fusion.41
  324.8 0.6 dynamic_slice.69
  326.1 4.7 %fusion.39 = f32[32,4,32,256]{3,0,2,1:T(8,128)S(1)} fusion(bf16[512,32,256]{2,0,1:T(8,128)(2,1)} %get-tuple-element.158, bf16[512,32,32]{0,1,2:T(8,128)(2,1)S(1)} %get-tuple-element.157, s32[]{:T(128)S(6)} %select_n.38), kind=kOutput, calls=%fused_computation.2.clone.1 | convolution fusion | flops 1073741824 | bytes 12713988 | tf_op jit(solution)/shard_map/while/body/eval_jaxpr/sci,sdj->ijcd/dot_general | solution.py:60
  330.8 8.3 %fusion.40 = bf16[4,256,32,32]{1,2,3,0:T(8,128)(2,1)S(1)} fusion(f32[32,4,32,256]{3,0,2,1:T(8,128)S(1)} %fusion.39, f32[4,256]{1,0:T(4,128)S(1)} %constant_dynamic-slice_fusion.2, bf16[1024,32,256]{2,0,1:T(8,128)(2,1)} %get-tuple-element.160, bf16[1024,32,32]{0,1,2:T(8,128)(2,1)S(1)} %get-tuple-element.159, s32[]{:T(128)S(6)} %select_n.38), kind=kOutput, calls=%fused_computation.5.clone.1 | convolution fusion | flops 2150629376 | bytes 23334916 | tf_op jit(solution)/shard_map/while/body/eval_jaxpr/sci,sdj->ijcd/dot_general | solution.py:63
  339.1 1.2 copy.35
  340.3 1.6 fusion.41
  343.1 4.7 %fusion.39 = f32[32,4,32,256]{3,0,2,1:T(8,128)S(1)} fusion(bf16[512,32,256]{2,0,1:T(8,128)(2,1)} %get-tuple-element.158, bf16[512,32,32]{0,1,2:T(8,128)(2,1)S(1)} %get-tuple-element.157, s32[]{:T(128)S(6)} %select_n.38), kind=kOutput, calls=%fused_computation.2.clone.1 | convolution fusion | flops 1073741824 | bytes 12713988 | tf_op jit(solution)/shard_map/while/body/eval_jaxpr/sci,sdj->ijcd/dot_general | solution.py:60
  347.8 8.3 %fusion.40 = bf16[4,256,32,32]{1,2,3,0:T(8,128)(2,1)S(1)} fusion(f32[32,4,32,256]{3,0,2,1:T(8,128)S(1)} %fusion.39, f32[4,256]{1,0:T(4,128)S(1)} %constant_dynamic-slice_fusion.2, bf16[1024,32,256]{2,0,1:T(8,128)(2,1)} %get-tuple-element.160, bf16[1024,32,32]{0,1,2:T(8,128)(2,1)S(1)} %get-tuple-element.159, s32[]{:T(128)S(6)} %select_n.38), kind=kOutput, calls=%fused_computation.5.clone.1 | convolution fusion | flops 2150629376 | bytes 23334916 | tf_op jit(solution)/shard_map/while/body/eval_jaxpr/sci,sdj->ijcd/dot_general | solution.py:63
  356.2 1.2 copy.35
  357.4 1.5 fusion.41
  360.2 4.7 %fusion.39 = f32[32,4,32,256]{3,0,2,1:T(8,128)S(1)} fusion(bf16[512,32,256]{2,0,1:T(8,128)(2,1)} %get-tuple-element.158, bf16[512,32,32]{0,1,2:T(8,128)(2,1)S(1)} %get-tuple-element.157, s32[]{:T(128)S(6)} %select_n.38), kind=kOutput, calls=%fused_computation.2.clone.1 | convolution fusion | flops 1073741824 | bytes 12713988 | tf_op jit(solution)/shard_map/while/body/eval_jaxpr/sci,sdj->ijcd/dot_general | solution.py:60
  364.8 8.3 %fusion.40 = bf16[4,256,32,32]{1,2,3,0:T(8,128)(2,1)S(1)} fusion(f32[32,4,32,256]{3,0,2,1:T(8,128)S(1)} %fusion.39, f32[4,256]{1,0:T(4,128)S(1)} %constant_dynamic-slice_fusion.2, bf16[1024,32,256]{2,0,1:T(8,128)(2,1)} %get-tuple-element.160, bf16[1024,32,32]{0,1,2:T(8,128)(2,1)S(1)} %get-tuple-element.159, s32[]{:T(128)S(6)} %select_n.38), kind=kOutput, calls=%fused_computation.5.clone.1 | convolution fusion | flops 2150629376 | bytes 23334916 | tf_op jit(solution)/shard_map/while/body/eval_jaxpr/sci,sdj->ijcd/dot_general | solution.py:63
  373.2 1.2 copy.35
  374.4 1.6 fusion.41
  377.2 4.7 %fusion.39 = f32[32,4,32,256]{3,0,2,1:T(8,128)S(1)} fusion(bf16[512,32,256]{2,0,1:T(8,128)(2,1)} %get-tuple-element.158, bf16[512,32,32]{0,1,2:T(8,128)(2,1)S(1)} %get-tuple-element.157, s32[]{:T(128)S(6)} %select_n.38), kind=kOutput, calls=%fused_computation.2.clone.1 | convolution fusion | flops 1073741824 | bytes 12713988 | tf_op jit(solution)/shard_map/while/body/eval_jaxpr/sci,sdj->ijcd/dot_general | solution.py:60
  381.9 8.3 %fusion.40 = bf16[4,256,32,32]{1,2,3,0:T(8,128)(2,1)S(1)} fusion(f32[32,4,32,256]{3,0,2,1:T(8,128)S(1)} %fusion.39, f32[4,256]{1,0:T(4,128)S(1)} %constant_dynamic-slice_fusion.2, bf16[1024,32,256]{2,0,1:T(8,128)(2,1)} %get-tuple-element.160, bf16[1024,32,32]{0,1,2:T(8,128)(2,1)S(1)} %get-tuple-element.159, s32[]{:T(128)S(6)} %select_n.38), kind=kOutput, calls=%fused_computation.5.clone.1 | convolution fusion | flops 2150629376 | bytes 23334916 | tf_op jit(solution)/shard_map/while/body/eval_jaxpr/sci,sdj->ijcd/dot_general | solution.py:63
  390.2 1.2 copy.35
  391.4 1.6 fusion.41
  393.0 3.8 fusion.16
  (42 shorter events, 3.7 us)
Async XLA Ops:
  6.5 5.2 %copy-start.1 = (bf16[64,32,256]{2,1,0:T(8,128)(2,1)S(1)}, bf16[64,32,256]{2,1,0:T(8,128)(2,1)}, u32[]{:S(2)}) copy-start(bf16[64,32,256]{2,1,0:T(8,128)(2,1)} %param.13) | copy-start | bytes 3145732
  6.5 6.8 %copy-start.2 = (bf16[256,32,32]{0,2,1:T(8,128)(2,1)S(1)}, bf16[256,32,32]{0,2,1:T(8,128)(2,1)}, u32[]{:S(2)}) copy-start(bf16[256,32,32]{0,2,1:T(8,128)(2,1)} %param.10) | copy-start | bytes 1572868
  6.5 10.2 %copy-start.5 = (s32[12]{0:T(128)S(1)}, s32[12]{0:T(128)}, u32[]{:S(2)}) copy-start(s32[12]{0:T(128)} %param.16) | copy-start | bytes 148
  6.5 10.6 %copy-start.4 = (s32[12]{0:T(128)S(1)}, s32[12]{0:T(128)}, u32[]{:S(2)}) copy-start(s32[12]{0:T(128)} %param.17) | copy-start | bytes 148
  6.5 44.8 %all-gather.6.cloned.1.call-start = ((), (), s32[]{:S(2)}) async-start(), calls=%async_computation.1 | async-start | bytes 3145728 | tf_op jit(solution)/shard_map/all_gather | solution.py:28
  9.5 119.9 %all-gather.4.cloned.1.call-start = ((), (), s32[]{:S(2)}) async-start(), calls=%async_computation | async-start | bytes 8912896 | tf_op jit(solution)/shard_map/all_gather | solution.py:31
  11.7 244.9 %all-gather.8.cloned.1.call-start = ((), (), s32[]{:S(2)}) async-start(), calls=%async_computation.2 | async-start | bytes 17825792 | tf_op jit(solution)/shard_map/all_gather | solution.py:32
  13.3 243.3 %copy-start = (bf16[1024,128]{1,0:T(8,128)(2,1)S(1)}, bf16[1024,128]{1,0:T(8,128)(2,1)}, u32[]{:S(2)}) copy-start(bf16[1024,128]{1,0:T(8,128)(2,1)} %param.14) | copy-start | bytes 786436
  13.7 22.6 %collective-permute-start = (bf16[256,32,32]{0,1,2:T(8,128)(2,1)S(1)}, bf16[256,32,32]{0,1,2:T(8,128)(2,1)S(1)}, u32[]{:S(2)}, u32[]{:S(2)}) collective-permute-start(bf16[256,32,32]{0,1,2:T(8,128)(2,1)S(1)} %copy.26), channel_id=1, source_target_pairs={{0,1},{1,0},{2,3},{3,2},{4,5},{5,4},{6,7},{7,6},{8,9},{9,8},{10,11... | collective-permute-start | bytes 1572872 | tf_op jit(solution)/shard_map/ppermute | solution.py:23
  256.6 136.3 %copy-start.3 = (f32[128]{0:T(128)S(1)}, f32[128]{0:T(128)}, u32[]{:S(2)}) copy-start(f32[128]{0:T(128)} %param.15) | copy-start | bytes 1540
Sparse Core Ops, SparseCore 0:
  9.6 41.6 all-gather.5
  53.5 75.7 all-gather.3
  131.6 125.0 all-gather.7
